TPU v7x, 16 devices: a 4x2x1 block of a 4x4x8 slice. The times are simulated.
16 devices in a mesh: rep: 4 (over y, z, core), dp: 4 (over x).
Axes of the slice: x: 4, y: 2, z: 1, core: 2. Of those that a mesh axis runs over, the one named last changes fastest.
The devices are a block of a 4x4x8 slice.
Arguments:
- x: bfloat16 [16, 4096, 896], P(('rep', 'dp')), parts along dimension 0
- dy: bfloat16 [16, 4096, 896], P(('rep', 'dp')), parts along dimension 0
- w_gate: bfloat16 [2, 896, 3584], P(None, 'dp')
- w_up: bfloat16 [2, 896, 3584], P(None, 'dp')
- w_down: bfloat16 [2, 3584, 896], P(None, 'dp')
Outputs:
- output 1: bfloat16 [16, 4096, 896], P(('rep', 'dp')), parts along dimension 0
- output 2: bfloat16 [8, 896, 3584], P('rep', 'dp'), parts along dimension 0
- output 3: bfloat16 [8, 896, 3584], P('rep', 'dp'), parts along dimension 0
- output 4: bfloat16 [8, 3584, 896], P('rep', 'dp'), parts along dimension 0
There are 4 independent parts. A program takes and returns all parts, laid end to end along the dimension named above; an argument that names none is the same for every part.
All inputs are finite; a program needn't handle non-finite values.
Results may differ from a plain program's by a relative error of at most 0.018.
Values are sent between devices in bfloat16 or wider.
A program may use at most 768 MiB of HBM per device.

v0:
```python
import jax
import jax.numpy as jnp
from jax import lax

NAMES = ("w_gate", "w_up", "w_down")


def matmul(a, w):
    return jnp.dot(a, w, preferred_element_type=jnp.float32).astype(jnp.bfloat16)


def normed(h):
    wide = h.astype(jnp.float32)
    scale = lax.rsqrt(jnp.mean(wide**2, -1, keepdims=True) + 1e-6)
    return (wide * scale).astype(jnp.bfloat16)


def layer(h, w):
    a = normed(h)
    gate = jnp.dot(a, w["w_gate"], preferred_element_type=jnp.float32)
    up = jnp.dot(a, w["w_up"], preferred_element_type=jnp.float32)
    return h + matmul((jax.nn.silu(gate) * up).astype(jnp.bfloat16), w["w_down"])


def stack(weights, h):
    for number in range(weights["w_gate"].shape[0]):
        h = layer(h, {name: w[number] for name, w in weights.items()})
    return h


def solution(mesh):
    groups = mesh.shape["rep"]

    def step(x, dy, *weights):
        shape = x.shape
        x, dy = (t.reshape(groups, -1, *t.shape[1:]) for t in (x, dy))

        def of_a_group(x, dy):
            _, back = jax.vjp(stack, dict(zip(NAMES, weights, strict=True)), x)
            by_weights, by_x = back(dy)
            return (by_x, *(by_weights[name] for name in NAMES))

        by_x, *by_weights = jax.vmap(of_a_group)(x, dy)
        return (by_x.reshape(shape), *(t.reshape(-1, *t.shape[2:]) for t in by_weights))

    return step
```

profile of v0, /device:TPU:112, one launch (start us, length us, event | category | flops | bytes accessed | tf_op | source)
XLA Modules:
  0.0 1319.4 jit_solution(11355316594562492334)
XLA Ops:
  23.9 10.8 copy.1
  35.3 10.8 copy
  46.0 31.0 %all-gather.30.cloned.1.call-done = bf16[1,896,3584]{2,1,0:T(8,128)(2,1)} async-done(((bf16[1,224,3584]{2,1,0:T(8,128)(2,1)}), bf16[1,896,3584]{2,1,0:T(8,128)(2,1)}) %all-gather.30.cloned.1.call-update) | async-done | bytes 6422544 | tf_op jit(solution)/vmap(jvp())/squeeze | solution.py:27
  77.0 39.8 %fusion.83 = f32[4096,3584]{1,0:T(8,128)} fusion(bf16[1,896,3584]{2,1,0:T(8,128)(2,1)} %all-gather.30.cloned.1.call-done, bf16[1,4096,896]{2,1,0:T(8,128)(2,1)} %param.1, f32[4096]{0:T(1024)S(1)} %get-tuple-element.13), kind=kOutput, calls=%fused_computation.99 | convolution fusion | flops 26317684736 | bytes 72499200 | tf_op jit(solution)/vmap(jvp())/dot_general | solution.py:20
  116.8 25.8 %all-gather.32.cloned.1.call-done = bf16[1,896,3584]{2,1,0:T(8,128)(2,1)} async-done(((bf16[1,224,3584]{2,1,0:T(8,128)(2,1)}), bf16[1,896,3584]{2,1,0:T(8,128)(2,1)}) %all-gather.32.cloned.1.call-update) | async-done | bytes 6422544 | tf_op jit(solution)/vmap(jvp())/squeeze | solution.py:27
  142.5 39.7 %fusion.79 = f32[4096,3584]{1,0:T(8,128)} fusion(bf16[1,896,3584]{2,1,0:T(8,128)(2,1)} %all-gather.32.cloned.1.call-done, bf16[1,4096,896]{2,1,0:T(8,128)(2,1)} %param.1, f32[4096]{0:T(1024)S(1)} %get-tuple-element.13), kind=kOutput, calls=%fused_computation.95 | convolution fusion | flops 26317684736 | bytes 72499200 | tf_op jit(solution)/vmap(jvp())/dot_general | solution.py:21
  182.2 46.9 %fusion.24 = bf16[4096,3584]{1,0:T(8,128)(2,1)} fusion(f32[4096,3584]{1,0:T(8,128)} %fusion.79, f32[4096,3584]{1,0:T(8,128)} %fusion.83), kind=kLoop, calls=%fused_computation.36 | loop fusion | flops 88080384 | bytes 146800640
  229.2 35.9 %fusion.40 = (f32[4096]{0:T(1024)S(1)}, bf16[1,1,4096,896]{2,3,1,0:T(8,128)(2,1)}) fusion(bf16[4096,3584]{1,0:T(8,128)(2,1)} %fusion.24, bf16[1,3584,896]{2,1,0:T(8,128)(2,1)} %all-gather.34.cloned.1.call-done, bf16[1,4096,896]{1,2,0:T(8,128)(2,1)} %copy.1), kind=kOutput, calls=%fused_computation.62 | convolution fusion | flops 26325020672 | bytes 50479104 | tf_op jit(solution)/vmap(jvp())/dot_general | solution.py:9
  272.9 40.0 %fusion.74 = f32[4096,3584]{1,0:T(8,128)} fusion(bf16[1,896,3584]{2,1,0:T(8,128)(2,1)} %all-gather.36.cloned.1.call-done, bf16[1,1,4096,896]{2,3,1,0:T(8,128)(2,1)} %get-tuple-element.15, f32[4096]{0:T(1024)S(1)} %bitcast.302), kind=kOutput, calls=%fused_computation.90 | convolution fusion | flops 26317684736 | bytes 72499200 | tf_op jit(solution)/vmap(jvp())/dot_general | solution.py:20
  312.9 25.4 %all-gather.40.cloned.1.call-done = bf16[1,896,3584]{2,1,0:T(8,128)(2,1)} async-done(((bf16[1,224,3584]{2,1,0:T(8,128)(2,1)}), bf16[1,896,3584]{2,1,0:T(8,128)(2,1)}) %all-gather.40.cloned.1.call-update) | async-done | bytes 6422544 | tf_op jit(solution)/vmap(jvp())/squeeze | solution.py:27
  338.3 40.2 %fusion.68 = f32[4096,3584]{1,0:T(8,128)} fusion(bf16[1,896,3584]{2,1,0:T(8,128)(2,1)} %all-gather.40.cloned.1.call-done, bf16[1,1,4096,896]{2,3,1,0:T(8,128)(2,1)} %get-tuple-element.15, f32[4096]{0:T(1024)S(1)} %bitcast.303), kind=kOutput, calls=%fused_computation.84 | convolution fusion | flops 26317684736 | bytes 72499200 | tf_op jit(solution)/vmap(jvp())/dot_general | solution.py:21
  378.5 24.6 %all-gather.38.cloned.1.call-done = bf16[1,3584,896]{2,1,0:T(8,128)(2,1)} async-done(((bf16[1,896,896]{2,1,0:T(8,128)(2,1)}), bf16[1,3584,896]{2,1,0:T(8,128)(2,1)}) %all-gather.38.cloned.1.call-update) | async-done | bytes 6422544 | tf_op jit(solution)/vmap(jvp())/squeeze | solution.py:27
  403.1 37.5 %convolution_convert_fusion.1 = bf16[4096,3584]{1,0:T(8,128)(2,1)} fusion(bf16[1,4096,896]{2,1,0:T(8,128)(2,1)} %param, bf16[1,3584,896]{2,1,0:T(8,128)(2,1)} %all-gather.38.cloned.1.call-done), kind=kOutput, calls=%fused_computation.35 | convolution fusion | flops 26321354752 | bytes 43122688 | tf_op jit(solution)/vmap(transpose(jvp()))/dot_general | solution.py:9
  440.6 59.3 %fusion.4 = bf16[4096,3584]{1,0:T(8,128)(2,1)} fusion(f32[4096,3584]{1,0:T(8,128)} %fusion.74, f32[4096,3584]{1,0:T(8,128)} %fusion.68, bf16[4096,3584]{1,0:T(8,128)(2,1)} %convolution_convert_fusion.1), kind=kLoop, calls=%fused_computation.10 | loop fusion | flops 176160768 | bytes 176160768
  499.9 31.8 %fusion.72 = bf16[4096,896]{0,1:T(8,128)(2,1)} fusion(bf16[4096,3584]{1,0:T(8,128)(2,1)} %fusion.4, bf16[1,896,3584]{2,1,0:T(8,128)(2,1)S(1)} %copy-done.12), kind=kOutput, calls=%fused_computation.88 | convolution fusion | flops 26306674688 | bytes 43122688 | tf_op jit(solution)/vmap(transpose(jvp()))/dot_general | solution.py:20
  531.7 41.1 %fusion.42 = (f32[4096]{0:T(1024)S(1)}, bf16[4096,896]{0,1:T(8,128)(2,1)}) fusion(bf16[1,1,4096,896]{2,3,1,0:T(8,128)(2,1)} %get-tuple-element.15, bf16[4096,896]{0,1:T(8,128)(2,1)} %fusion.72, bf16[1,896,3584]{2,1,0:T(8,128)(2,1)S(1)} %bitcast.315, bf16[4096,3584]{1,0:T(8,128)(2,1)} %convolution_convert_fusion.1, f32[4096,3584]{1,0:T(8,128)} %fusion.74), kind=kOutput, calls=%fused_computation.64 | convolution fusion | flops 26416771072 | bytes 116539392 | tf_op jit(solution)/vmap(transpose(jvp()))/dot_general | solution.py:21
  572.8 10.8 fusion.56
  583.6 38.3 %convolution_bitcast_fusion = f32[1,3584,896]{2,1,0:T(8,128)} fusion(bf16[4096,3584]{1,0:T(8,128)(2,1)} %fusion.24, bf16[1,1,4096,896]{2,3,1,0:T(8,128)(2,1)} %fusion.56), kind=kOutput, calls=%fused_computation.68 | convolution fusion | flops 26306674688 | bytes 49545216 | tf_op jit(solution)/vmap(transpose(jvp()))/dot_general | solution.py:9
  622.1 49.0 %fusion.43 = f32[1,3584,896]{2,1,0:T(8,128)} fusion(f32[4096,3584]{1,0:T(8,128)} %fusion.68, f32[4096,3584]{1,0:T(8,128)} %fusion.74, bf16[1,4096,896]{2,1,0:T(8,128)(2,1)} %param), kind=kOutput, calls=%fused_computation.65 | convolution fusion | flops 26394755072 | bytes 137625600 | tf_op jit(solution)/vmap(transpose(jvp()))/dot_general | solution.py:9
  671.2 37.8 %convolution_convert_fusion = bf16[4096,3584]{1,0:T(8,128)(2,1)} fusion(bf16[1,1,4096,896]{2,3,1,0:T(8,128)(2,1)} %fusion.56, bf16[1,3584,896]{2,1,0:T(8,128)(2,1)} %all-gather.34.cloned.1.call-done), kind=kOutput, calls=%fused_computation.34 | convolution fusion | flops 26321354752 | bytes 43122688 | tf_op jit(solution)/vmap(transpose(jvp()))/dot_general | solution.py:9
  709.0 58.4 %fusion.7 = bf16[4096,3584]{1,0:T(8,128)(2,1)} fusion(f32[4096,3584]{1,0:T(8,128)} %fusion.83, f32[4096,3584]{1,0:T(8,128)} %fusion.79, bf16[4096,3584]{1,0:T(8,128)(2,1)} %convolution_convert_fusion), kind=kLoop, calls=%fused_computation.13 | loop fusion | flops 176160768 | bytes 176160768
  767.4 41.1 %fusion.46 = f32[1,896,3584]{2,1,0:T(8,128)} fusion(bf16[4096,3584]{1,0:T(8,128)(2,1)} %convolution_convert_fusion.1, f32[4096,3584]{1,0:T(8,128)} %fusion.74, bf16[1,1,4096,896]{2,3,1,0:T(8,128)(2,1)S(1)} %copy-done.2, f32[4096]{0:T(1024)S(1)} %bitcast.305), kind=kOutput, calls=%fused_computation.66 | convolution fusion | flops 26405765120 | bytes 108281856 | tf_op jit(solution)/vmap(transpose(jvp()))/dot_general | solution.py:21
  808.7 33.8 %fusion.81 = bf16[4096,896]{0,1:T(8,128)(2,1)} fusion(bf16[4096,3584]{1,0:T(8,128)(2,1)} %fusion.7, bf16[1,896,3584]{2,1,0:T(8,128)(2,1)} %all-gather.30.cloned.1.call-done), kind=kOutput, calls=%fused_computation.97 | convolution fusion | flops 26306674688 | bytes 43122688 | tf_op jit(solution)/vmap(transpose(jvp()))/dot_general | solution.py:20
  842.5 42.4 %fusion.38 = (f32[4096]{0:T(1024)S(1)}, bf16[4096,896]{0,1:T(8,128)(2,1)}) fusion(bf16[1,4096,896]{1,2,0:T(8,128)(2,1)S(1)} %copy-done, bf16[4096,896]{0,1:T(8,128)(2,1)} %fusion.81, bf16[1,896,3584]{2,1,0:T(8,128)(2,1)} %all-gather.32.cloned.1.call-done, bf16[4096,3584]{1,0:T(8,128)(2,1)} %convolution_convert_fusion, f32[4096,3584]{1,0:T(8,128)} %fusion.83), kind=kOutput, calls=%fused_computation.60 | convolution fusion | flops 26416771072 | bytes 116539392 | tf_op jit(solution)/vmap(transpose(jvp()))/dot_general | solution.py:21
  885.6 41.3 %fusion.49 = f32[1,896,3584]{2,1,0:T(8,128)} fusion(bf16[4096,3584]{1,0:T(8,128)(2,1)} %convolution_convert_fusion, f32[4096,3584]{1,0:T(8,128)} %fusion.83, bf16[1,4096,896]{1,2,0:T(8,128)(2,1)S(1)} %copy-done, f32[4096]{0:T(1024)S(1)} %bitcast.307), kind=kOutput, calls=%fused_computation.67 | convolution fusion | flops 26405765120 | bytes 108281856 | tf_op jit(solution)/vmap(transpose(jvp()))/dot_general | solution.py:21
  927.1 33.4 %convolution_bitcast_fusion.2 = f32[1,896,3584]{2,1,0:T(8,128)} fusion(bf16[4096,3584]{1,0:T(8,128)(2,1)} %fusion.4, bf16[1,1,4096,896]{2,3,1,0:T(8,128)(2,1)} %get-tuple-element.15, f32[4096]{0:T(1024)S(1)} %bitcast.306), kind=kOutput, calls=%fused_computation.70 | convolution fusion | flops 26317684736 | bytes 49561600 | tf_op jit(solution)/vmap(transpose(jvp()))/dot_general | solution.py:20
  960.7 33.5 %convolution_bitcast_fusion.1 = f32[1,896,3584]{2,1,0:T(8,128)} fusion(bf16[4096,3584]{1,0:T(8,128)(2,1)} %fusion.7, bf16[1,4096,896]{1,2,0:T(8,128)(2,1)} %copy.1, f32[4096]{0:T(1024)S(1)} %bitcast.308), kind=kOutput, calls=%fused_computation.69 | convolution fusion | flops 26317684736 | bytes 49561600 | tf_op jit(solution)/vmap(transpose(jvp()))/dot_general | solution.py:20
  994.3 12.3 fusion.55
  1006.6 10.8 copy.2
  1025.6 53.6 %reduce-scatter.25.cloned.1.call-done = f32[1,224,3584]{2,1,0:T(8,128)} async-done(((f32[1,896,3584]{2,1,0:T(8,128)}), f32[1,224,3584]{2,1,0:T(8,128)}) %reduce-scatter.25.cloned.1.call-update) | async-done | bytes 3211280
  1083.2 110.7 %reduce-scatter.19.cloned.1.call-done = f32[1,224,3584]{2,1,0:T(8,128)} async-done(((f32[1,896,3584]{2,1,0:T(8,128)}), f32[1,224,3584]{2,1,0:T(8,128)}) %reduce-scatter.19.cloned.1.call-update) | async-done | bytes 3211280
  1196.0 112.4 %reduce-scatter.21.cloned.1.call-done = f32[1,224,3584]{2,1,0:T(8,128)} async-done(((f32[1,896,3584]{2,1,0:T(8,128)}), f32[1,224,3584]{2,1,0:T(8,128)}) %reduce-scatter.21.cloned.1.call-update) | async-done | bytes 3211280
  (78 shorter events, 44.7 us)
Async XLA Ops:
  7.2 8.1 copy-start.3
  7.2 69.8 %all-gather.30.cloned.1.call-start = ((), (), s32[]{:S(2)}) async-start(), calls=%async_computation.6 | async-start | bytes 8028160 | tf_op jit(solution)/vmap(jvp())/squeeze | solution.py:27
  11.3 131.3 %all-gather.32.cloned.1.call-start = ((), (), s32[]{:S(2)}) async-start(), calls=%async_computation.7 | async-start | bytes 8028160 | tf_op jit(solution)/vmap(jvp())/squeeze | solution.py:27
  15.2 214.0 %all-gather.34.cloned.1.call-start = ((), (), s32[]{:S(2)}) async-start(), calls=%async_computation.8 | async-start | bytes 8028160 | tf_op jit(solution)/vmap(jvp())/squeeze | solution.py:27
  17.3 255.6 %all-gather.36.cloned.1.call-start = ((), (), s32[]{:S(2)}) async-start(), calls=%async_computation.9 | async-start | bytes 8028160 | tf_op jit(solution)/vmap(jvp())/squeeze | solution.py:27
  18.0 320.3 %all-gather.40.cloned.1.call-start = ((), (), s32[]{:S(2)}) async-start(), calls=%async_computation.11 | async-start | bytes 8028160 | tf_op jit(solution)/vmap(jvp())/squeeze | solution.py:27
  18.6 384.5 %all-gather.38.cloned.1.call-start = ((), (), s32[]{:S(2)}) async-start(), calls=%async_computation.10 | async-start | bytes 8028160 | tf_op jit(solution)/vmap(jvp())/squeeze | solution.py:27
  19.2 998.1 %reduce-scatter.29.cloned.1.call-start = ((), (), s32[]{:S(2)}) async-start(), calls=%async_computation.17 | async-start | bytes 16056320
  265.0 0.6 copy-start.4
  265.7 72.6 %copy-start.6 = (f32[1,1,4096]{2,1,0:T(1,128)}, f32[1,1,4096]{2,1,0:T(1,128)S(1)}, u32[]{:S(2)}) copy-start(f32[1,1,4096]{2,1,0:T(1,128)S(1)} %rsqrt.23) | copy-start | bytes 49156
  440.6 59.3 %copy-start.12 = (bf16[1,896,3584]{2,1,0:T(8,128)(2,1)S(1)}, bf16[1,896,3584]{2,1,0:T(8,128)(2,1)}, u32[]{:S(2)}) copy-start(bf16[1,896,3584]{2,1,0:T(8,128)(2,1)} %all-gather.36.cloned.1.call-done) | copy-start | bytes 19267588
  440.6 91.1 %slice-start = ((s8[6422528]{0:T(1024)(128)(4,1)}), s8[4194304]{0:T(1024)(128)(4,1)S(1)}, s32[]{:S(2)}) async-start(s8[6422528]{0:T(1024)(128)(4,1)} %bitcast.314), calls=%async_computation.18 | async-start | bytes 8388608
  499.9 31.8 %slice-start.1 = ((s8[6422528]{0:T(1024)(128)(4,1)}), s8[2228224]{0:T(1024)(128)(4,1)S(1)}, s32[]{:S(2)}) async-start(s8[6422528]{0:T(1024)(128)(4,1)} %bitcast.314), calls=%async_computation.19 | async-start | bytes 4456448
  531.7 41.1 %copy-start.5 = (f32[4096]{0:T(1024)S(1)}, f32[4096]{0:T(1024)}, u32[]{:S(2)}) copy-start(f32[4096]{0:T(1024)} %copy-done.4) | copy-start | bytes 49156
  531.7 41.1 %copy-start.1 = (bf16[1,4096,896]{1,2,0:T(8,128)(2,1)S(1)}, bf16[1,4096,896]{1,2,0:T(8,128)(2,1)}, u32[]{:S(2)}) copy-start(bf16[1,4096,896]{1,2,0:T(8,128)(2,1)} %copy) | copy-start | bytes 22020100
  531.7 41.1 %copy-start.7 = (f32[1,1,4096]{2,1,0:T(1,128)S(1)}, f32[1,1,4096]{2,1,0:T(1,128)}, u32[]{:S(2)}) copy-start(f32[1,1,4096]{2,1,0:T(1,128)} %copy-done.6) | copy-start | bytes 49156
  622.0 397.5 %reduce-scatter.27.cloned.1.call-start = ((), (), s32[]{:S(2)}) async-start(), calls=%async_computation.16 | async-start | bytes 16056320
  671.1 352.4 %reduce-scatter.23.cloned.1.call-start = ((), (), s32[]{:S(2)}) async-start(), calls=%async_computation.14 | async-start | bytes 16056320
  709.0 58.4 %copy-start.2 = (bf16[1,1,4096,896]{2,3,1,0:T(8,128)(2,1)S(1)}, bf16[1,1,4096,896]{2,3,1,0:T(8,128)(2,1)}, u32[]{:S(2)}) copy-start(bf16[1,1,4096,896]{2,3,1,0:T(8,128)(2,1)} %get-tuple-element.15) | copy-start | bytes 22020100
  709.0 58.4 %copy-start.8 = (f32[1,1,4096]{2,1,0:T(1,128)S(1)}, f32[1,1,4096]{2,1,0:T(1,128)}, u32[]{:S(2)}) copy-start(f32[1,1,4096]{2,1,0:T(1,128)} %copy-done.6) | copy-start | bytes 49156
  808.6 270.7 %reduce-scatter.25.cloned.1.call-start = ((), (), s32[]{:S(2)}) async-start(), calls=%async_computation.15 | async-start | bytes 16056320
  808.7 33.9 %copy-start = (bf16[1,4096,896]{1,2,0:T(8,128)(2,1)S(1)}, bf16[1,4096,896]{1,2,0:T(8,128)(2,1)}, u32[]{:S(2)}) copy-start(bf16[1,4096,896]{1,2,0:T(8,128)(2,1)} %copy.1) | copy-start | bytes 22020100
  842.5 42.5 %copy-start.11 = (f32[4096]{0:T(1024)S(1)}, f32[4096]{0:T(1024)}, u32[]{:S(2)}) copy-start(f32[4096]{0:T(1024)} %get-tuple-element.12) | copy-start | bytes 49156
  885.6 41.5 %copy-start.9 = (f32[1,1,4096]{2,1,0:T(1,128)S(1)}, f32[1,1,4096]{2,1,0:T(1,128)}, u32[]{:S(2)}) copy-start(f32[1,1,4096]{2,1,0:T(1,128)} %copy-done.6) | copy-start | bytes 49156
  927.0 266.9 %reduce-scatter.19.cloned.1.call-start = ((), (), s32[]{:S(2)}) async-start(), calls=%async_computation.12 | async-start | bytes 16056320
  960.6 33.7 %copy-start.10 = (f32[1,1,4096]{2,1,0:T(1,128)S(1)}, f32[1,1,4096]{2,1,0:T(1,128)}, u32[]{:S(2)}) copy-start(f32[1,1,4096]{2,1,0:T(1,128)} %get-tuple-element.11) | copy-start | bytes 49156
  960.6 347.8 %reduce-scatter.21.cloned.1.call-start = ((), (), s32[]{:S(2)}) async-start(), calls=%async_computation.13 | async-start | bytes 16056320
Sparse Core Ops, SparseCore 0:
  11.4 65.5 all-gather.29
  79.1 63.3 all-gather.31
  144.1 63.3 all-gather.33
  209.5 63.3 all-gather.35
  274.9 63.3 all-gather.39
  339.7 63.3 all-gather.37
  622.1 113.2 reduce-scatter.28
  737.7 112.2 reduce-scatter.26
  852.4 112.2 reduce-scatter.22
  966.9 112.2 reduce-scatter.24
  1081.6 112.2 reduce-scatter.18
  1196.1 112.2 reduce-scatter.20
where the time goes:
time: 1330 us; the launch traced here: 1320 us
  matrix products  657 us (49%)
  waiting for transfers between devices  393 us (30%)
  other arithmetic  212 us (16%)
  local copies, waits for them, and re-layouts  42.8 us (3%)
  between operations  14.6 us (1%)
    unnamed x18, waiting for transfers between devices  279 us
    dot_general x6, matrix products, layer(): up = jnp.dot(a, w['w_up'], preferred_element_type=jnp.float32)  246 us
    dot_general x6, matrix products, layer(): gate = jnp.dot(a, w['w_gate'], preferred_element_type=jnp.float32)  212 us
    dot_general x5, matrix products, matmul(): jnp.dot(a, w, preferred_element_type=jnp.float32).astype(jnp.bfloat16)  199 us
    unnamed x4, other arithmetic  165 us
    squeeze x6, waiting for transfers between devices, stack(): h = layer(h, {name: w[number] for name, w in weights.items()})  114 us
    unnamed x33, local copies, waits for them, and re-layouts  33 us
  transfers between devices with their start and end apart: 12, of which 8 were waited for; matrix products, arithmetic and copies ran while one was open for 52% of the time, Pallas kernels for 0%

commit v1 on v0

v1 whole, which is shorter than its diff:
```python
import functools

import jax
import jax.numpy as jnp
from jax import lax
from jax.experimental import pallas as pl
from jax.experimental.pallas import tpu as pltpu
from jax.sharding import PartitionSpec as P

MESH = pl.DeviceIdType.MESH
BF, F32 = jnp.bfloat16, jnp.float32
LANES = 128
TILE = 1024
SMALL = 512
CHUNK = 256
EPS = 1e-6


def nn(a, b):
    return jnp.dot(a, b, preferred_element_type=F32)


def nt(a, b):
    return lax.dot_general(a, b, (((1,), (1,)), ((), ())), preferred_element_type=F32)


def sigmoid(g):
    return 1.0 / (1.0 + jnp.exp(-g))


def gated_back(g, u, d):
    s = sigmoid(g)
    silu = g * s
    d = d.astype(BF).astype(F32)
    return (silu * u).astype(BF), ((d * u) * (s + silu * (1.0 - s))).astype(BF), (d * silu).astype(BF)


def kernel(
    n, x, dy, wg, wu, wd,
    dx, og, ou, od, a1, a1t, dyt, h1, a2, a2t, dh1, dh1t, g1, u1, gw, gd,
    total, acc_w, acc_d, wgu, wdb, wdt, rows_a, rows_d, cols_a, cols_d, g_buf, u_buf, act, dgu,
    s1_w, s1_d, r1_w, r1_d, s2_w, s2_d, r2_w, r2_d, out_w, out_d,
    ag_send, ag_recv, load_sem, stream_sem, gu_sem, phase_sem, rs_send, rs_recv, out_sem,
):
    tokens, width = x.shape
    layers, depth, ff = wg.shape
    span = n * LANES
    share = ff // n
    blocks = ff // span
    tiles, smalls = tokens // TILE, tokens // SMALL
    half, dhalf = depth // 2, LANES // 2
    gathers = layers * blocks
    me = lax.axis_index("dp")
    rep = lax.axis_index("rep")
    core = rep % 2
    mate = rep + 1 - 2 * core
    right, left, across = (me + 1) % n, (me + n - 1) % n, (me + 2) % n
    to_right, to_left, to_mate = {"dp": right}, {"dp": left}, {"rep": mate}

    def aligned(v, m):
        return pl.multiple_of(v, m)

    def w_rows(owner, c):
        return pl.ds(aligned(owner * depth + c * half, 16), half)

    def d_rows(owner, c):
        return pl.ds(aligned(owner * LANES + c * dhalf, 16), dhalf)

    def remote(src, dst, send, recv, to):
        return pltpu.make_async_remote_copy(src_ref=src, dst_ref=dst, send_sem=send, recv_sem=recv, device_id=to, device_id_type=MESH)

    def wait_like(ref, sem):
        pltpu.make_async_copy(ref, ref, sem).wait()

    def sends_done(k, m):
        i = m % 4
        if k < 2:
            wait_like(gw.at[m, :, w_rows(me, core), :], ag_send.at[k, 0, i])
            wait_like(gd.at[m, d_rows(me, core), :], ag_send.at[k, 1, i])
        elif k < 4:
            wait_like(gw.at[m, :, w_rows(me, core), pl.ds(0, span // 2)], ag_send.at[k, 0, i])
            wait_like(gd.at[m, pl.ds(0, dhalf // 2), :], ag_send.at[k, 1, i])
        else:
            wait_like(gw.at[m, :, pl.ds(0, 3 * half), :], ag_send.at[k, 0, i])
            wait_like(gd.at[m, pl.ds(0, 3 * dhalf), :], ag_send.at[k, 1, i])

    def give(m):
        layer, b = m // blocks, m % blocks

        @pl.when(m >= 4)
        def _():
            sends_done(0, m - 4)
            sends_done(1, m - 4)

        i = m % 4
        for k, to in ((0, to_right), (1, to_left)):
            for j, w in enumerate((wg, wu)):
                for group in range(n):
                    at = pl.ds(aligned(group * share + b * LANES, LANES), LANES)
                    remote(
                        w.at[layer, pl.ds(aligned(core * half, 16), half), at],
                        gw.at[m, j, w_rows(me, core), pl.ds(group * LANES, LANES)],
                        ag_send.at[k, 0, i], ag_recv.at[k, 0, m], to,
                    ).start()
            remote(
                wd.at[layer, pl.ds(aligned(b * LANES + core * dhalf, 16), dhalf), :],
                gd.at[m, d_rows(me, core), :],
                ag_send.at[k, 1, i], ag_recv.at[k, 1, m], to,
            ).start()

    def swap(m, owner):
        w, d = gw.at[m, :, w_rows(owner, core), :], gd.at[m, d_rows(owner, core), :]
        remote(w, w, ag_send.at[4, 0, m % 4], ag_recv.at[4, 0, m], to_mate).start()
        remote(d, d, ag_send.at[4, 1, m % 4], ag_recv.at[4, 1, m], to_mate).start()

    def pass_on(m):
        i = m % 4

        @pl.when(m >= 4)
        def _():
            for k in (2, 3, 4):
                sends_done(k, m - 4)

        for k, owner in ((0, left), (1, right)):
            wait_like(gw.at[m, :, w_rows(owner, core), :], ag_recv.at[k, 0, m])
            wait_like(gd.at[m, d_rows(owner, core), :], ag_recv.at[k, 1, m])
        for k, owner, to, part in ((2, left, to_right, 0), (3, right, to_left, 1)):
            w = gw.at[m, :, w_rows(owner, core), pl.ds(part * (span // 2), span // 2)]
            d = gd.at[m, pl.ds(aligned(owner * LANES + core * dhalf + part * (dhalf // 2), 16), dhalf // 2), :]
            remote(w, w, ag_send.at[k, 0, i], ag_recv.at[k, 0, m], to).start()
            remote(d, d, ag_send.at[k, 1, i], ag_recv.at[k, 1, m], to).start()
        swap(m, left)
        swap(m, right)

    def pass_across(m):
        for k, part in ((2, 0), (3, 1)):
            wait_like(gw.at[m, :, w_rows(across, core), pl.ds(part * (span // 2), span // 2)], ag_recv.at[k, 0, m])
            wait_like(gd.at[m, pl.ds(aligned(across * LANES + core * dhalf + part * (dhalf // 2), 16), dhalf // 2), :], ag_recv.at[k, 1, m])
        swap(m, across)

    def gathered(m):
        wait_like(gw.at[m, :, pl.ds(0, 3 * half), :], ag_recv.at[4, 0, m])
        wait_like(gd.at[m, pl.ds(0, 3 * dhalf), :], ag_recv.at[4, 1, m])

    def load(m, slot):
        layer, b = m // blocks, m % blocks
        for owner in (left, right, across):
            r, d = pl.ds(aligned(owner * depth, 32), depth), pl.ds(aligned(owner * LANES, LANES), LANES)
            pltpu.make_async_copy(gw.at[m, :, r, :], wgu.at[slot, :, r, :], load_sem.at[0]).start()
            pltpu.make_async_copy(gd.at[m, d, :], wdb.at[d, :], load_sem.at[1]).start()
        r = pl.ds(aligned(me * depth, 32), depth)
        for j, w in enumerate((wg, wu)):
            for group in range(n):
                at = pl.ds(aligned(group * share + b * LANES, LANES), LANES)
                pltpu.make_async_copy(
                    w.at[layer, :, at], wgu.at[slot, j, r, pl.ds(group * LANES, LANES)], load_sem.at[0]
                ).start()
        pltpu.make_async_copy(
            wd.at[layer, pl.ds(aligned(b * LANES, LANES), LANES), :],
            wdb.at[pl.ds(aligned(me * LANES, LANES), LANES), :], load_sem.at[1],
        ).start()

    def loaded(slot):
        wait_like(wgu.at[slot], load_sem.at[0])
        wait_like(wdb, load_sem.at[1])
        for c in range(span // LANES):
            at = pl.ds(c * LANES, LANES)
            wdt[:, at] = wdb[at, :].T

    def gather_ticks(m, t):
        more = m + 1 < gathers

        @pl.when((t == 0) & more)
        def _():
            pass_on(m + 1)

        @pl.when((t == 0) & (m < blocks))
        def _():
            give(m + 3)

        @pl.when((t == 0) & (m == blocks))
        def _():
            lax.fori_loop(blocks + 3, gathers, lambda k, _: give(k), None)

        @pl.when((t == 2) & more)
        def _():
            pass_across(m + 1)

        @pl.when(t == 3)
        def _():
            @pl.when(more)
            def _():
                gathered(m + 1)

            load((m + 1) % gathers, (m + 1) % 2)

    def own_w(p, j, owner, part=None):
        at = slice(None) if part is None else pl.ds(part * (span // 2), span // 2)
        return acc_w[p, j, pl.ds(aligned(owner * depth, 32), depth), at]

    def own_d(p, owner, part=None):
        at = slice(None) if part is None else pl.ds(part * (width // 2), width // 2)
        return acc_d[p, at, pl.ds(aligned(owner * LANES, LANES), LANES)]

    def w_half(ref, part):
        return ref.at[:, :, pl.ds(part * (span // 2), span // 2)]

    def d_half(ref, part):
        return ref.at[pl.ds(part * (width // 2), width // 2), :]

    def first_copies():
        for part, to in ((0, to_right), (1, to_left)):
            yield remote(w_half(s1_w, part), w_half(r1_w, part), rs_send.at[0, part, 0], rs_recv.at[0, part, 0], to)
            yield remote(d_half(s1_d, part), d_half(r1_d, part), rs_send.at[0, part, 1], rs_recv.at[0, part, 1], to)

    def second_copies():
        for part, to in ((0, to_right), (1, to_left)):
            yield remote(s2_w.at[part], r2_w.at[part], rs_send.at[1, part, 0], rs_recv.at[1, part, 0], to)
            yield remote(s2_d.at[part], r2_d.at[part], rs_send.at[1, part, 1], rs_recv.at[1, part, 1], to)

    def reduce_start(r):
        p = r % 2
        for j in range(2):
            s1_w[j] = own_w(p, j, across).astype(BF)
        s1_d[...] = own_d(p, across).astype(BF)
        for copy in first_copies():
            copy.start()

    def reduce_middle(r):
        p = r % 2
        for copy in first_copies():
            copy.wait()
        for part, owner in ((0, right), (1, left)):
            for j in range(2):
                came, plain = pl.ds(part * (span // 2), span // 2), pl.ds((1 - part) * (span // 2), span // 2)
                s2_w[part, j, :, came] = (own_w(p, j, owner, part) + r1_w[j, :, came].astype(F32)).astype(BF)
                s2_w[part, j, :, plain] = own_w(p, j, owner, 1 - part).astype(BF)
            came, plain = pl.ds(part * (width // 2), width // 2), pl.ds((1 - part) * (width // 2), width // 2)
            s2_d[part, came, :] = (own_d(p, owner, part) + r1_d[came, :].astype(F32)).astype(BF)
            s2_d[part, plain, :] = own_d(p, owner, 1 - part).astype(BF)
        for copy in second_copies():
            copy.start()

    def result_copies(r):
        layer, b = layers - 1 - r // blocks, r % blocks
        for j, o in enumerate((og, ou)):
            for group in range(n):
                at = pl.ds(aligned(group * share + b * LANES, LANES), LANES)
                yield pltpu.make_async_copy(out_w.at[j, :, pl.ds(group * LANES, LANES)], o.at[layer, :, at], out_sem.at[j, group])
        yield pltpu.make_async_copy(out_d, od.at[layer, pl.ds(aligned(b * LANES, LANES), LANES), :], out_sem.at[2, 0])

    def reduce_end(r):
        p = r % 2
        for copy in second_copies():
            copy.wait()

        @pl.when(r >= 1)
        def _():
            for copy in result_copies(r - 1):
                copy.wait()

        for j in range(2):
            out_w[j] = (own_w(p, j, me) + r2_w[0, j].astype(F32) + r2_w[1, j].astype(F32)).astype(BF)
        mine = (own_d(p, me) + r2_d[0].astype(F32) + r2_d[1].astype(F32)).astype(BF)
        out_d[...] = mine.T
        for copy in result_copies(r):
            copy.start()

    def token_rows(ref, t, size):
        return ref.at[pl.ds(aligned(t * size, size), size), :]

    def token_cols(ref, t, size):
        return ref.at[:, pl.ds(aligned(t * size, size), size)]

    def copies(pairs, slot):
        for k, (src, dst) in enumerate(pairs):
            yield pltpu.make_async_copy(src, dst, stream_sem.at[k, slot])

    def start(pairs, slot):
        for copy in copies(pairs, slot):
            copy.start()

    def wait(pairs, slot):
        for copy in copies(pairs, slot):
            copy.wait()

    def norm_scale(wide):
        return lax.rsqrt(jnp.sum(wide * wide, -1, keepdims=True) * (1.0 / width) + EPS)

    def norm_back(h, da):
        wide = h.astype(F32)
        scale = norm_scale(wide)
        inner = jnp.sum(da * wide, -1, keepdims=True)
        return da * scale - wide * (scale * scale * scale * inner * (1.0 / width))

    def passes(ins, outs, chunk, between=()):
        def put(t, slot):
            for k, (src, dst) in enumerate(outs(t, slot)):
                yield pltpu.make_async_copy(src, dst, phase_sem.at[k, slot])

        start(ins(0, 0), 0)
        for t in range(tiles):
            slot = t % 2
            if t >= 1:
                for copy in put(t - 1, 1 - slot):
                    copy.wait()
            if t + 1 < tiles:
                start(ins(t + 1, 1 - slot), 1 - slot)
            wait(ins(t, slot), slot)

            def one(c, _):
                at = pl.ds(aligned(c * LANES, LANES), LANES)
                chunk(slot, at, pl.ds(aligned(t * TILE + c * LANES, LANES), LANES))

            lax.fori_loop(0, TILE // LANES, one, None)
            for copy in put(t, slot):
                copy.start()
            for after, act_ in between:
                if after == t:
                    act_()
        for copy in put(tiles - 1, (tiles - 1) % 2):
            copy.wait()

    barrier = pltpu.get_barrier_semaphore()
    for to in (to_right, to_left, to_mate):
        pl.semaphore_signal(barrier, inc=1, device_id=to, device_id_type=MESH)
    pl.semaphore_wait(barrier, 3)
    give(0)

    def enter(slot, at, _):
        wide = rows_a[slot, at, :].astype(F32)
        a = (wide * norm_scale(wide)).astype(BF)
        rows_a[slot, at, :] = a
        cols_a[slot, :, at] = a.T
        cols_d[slot, :, at] = rows_d[slot, at, :].T

    def first_pass():
        pass_on(0)
        give(1)
        give(2)

    def first_load():
        gathered(0)
        load(0, 0)

    passes(
        lambda t, s: [(token_rows(x, t, TILE), rows_a.at[s]), (token_rows(dy, t, TILE), rows_d.at[s])],
        lambda t, s: [
            (rows_a.at[s], token_rows(a1, t, TILE)), (cols_a.at[s], token_cols(a1t, t, TILE)), (cols_d.at[s], token_cols(dyt, t, TILE)),
        ],
        enter,
        [(1, first_pass), (2, lambda: pass_across(0)), (3, first_load)],
    )

    def add_total(at, first, value):
        total[:, at] = value + jnp.where(first, 0.0, total[:, at])

    def f1_in(s, slot):
        return [(token_rows(a1, s % tiles, TILE), rows_a.at[slot])]

    def gu_copies(m, t, h):
        at = pl.ds(aligned(t * TILE + h * SMALL, SMALL), SMALL)
        yield pltpu.make_async_copy(g_buf.at[h], g1.at[m, at, :], gu_sem.at[0, h])
        yield pltpu.make_async_copy(u_buf.at[h], u1.at[m, at, :], gu_sem.at[1, h])

    def f1_step(s, _):
        m, t, slot = s // tiles, s % tiles, s % 2
        gather_ticks(m, t)

        @pl.when(t == 0)
        def _():
            loaded(m % 2)

        @pl.when(s + 1 < blocks * tiles)
        def _():
            start(f1_in(s + 1, 1 - slot), 1 - slot)

        wait(f1_in(s, slot), slot)
        w = wgu.at[m % 2]
        for h in range(TILE // SMALL):
            @pl.when(s > 0)
            def _():
                for copy in gu_copies(m, t, h):
                    copy.wait()

            for c in range(SMALL // CHUNK):
                r, own = pl.ds(h * SMALL + c * CHUNK, CHUNK), pl.ds(c * CHUNK, CHUNK)
                a = rows_a[slot, r, :]
                g, u = nn(a, w[0]), nn(a, w[1])
                g_buf[h, own, :] = g
                u_buf[h, own, :] = u
                act[r, :] = (g * sigmoid(g) * u).astype(BF)
            for copy in gu_copies(m, t, h):
                copy.start()
        add_total(pl.ds(aligned(t * TILE, TILE), TILE), m == 0, nt(wdt[...], act[...]))

    start(f1_in(0, 0), 0)
    lax.fori_loop(0, blocks * tiles, f1_step, None)
    for h in range(TILE // SMALL):
        for copy in gu_copies(blocks - 1, tiles - 1, h):
            copy.wait()

    def turn(slot, at, tok):
        h = rows_d[slot, at, :].astype(F32) + total[:, tok].astype(BF).T.astype(F32)
        h = h.astype(BF)
        rows_d[slot, at, :] = h
        wide = h.astype(F32)
        a = (wide * norm_scale(wide)).astype(BF)
        rows_a[slot, at, :] = a
        cols_a[slot, :, at] = a.T

    passes(
        lambda t, s: [(token_rows(x, t, TILE), rows_d.at[s])],
        lambda t, s: [
            (rows_d.at[s], token_rows(h1, t, TILE)), (rows_a.at[s], token_rows(a2, t, TILE)), (cols_a.at[s], token_cols(a2t, t, TILE)),
        ],
        turn,
    )

    def fold(p, tok, size, first_step, first_block, slot, w):
        r = pl.ds(0, size)
        add_total(tok, first_block, nt(w[0], dgu[0, r, :]) + nt(w[1], dgu[1, r, :]))
        for j in range(2):
            acc_w[p, j] = nn(cols_a[slot, :, r], dgu[j, r, :]) + jnp.where(first_step, 0.0, acc_w[p, j])
        acc_d[p] = nn(cols_d[slot, :, r], act[r, :]) + jnp.where(first_step, 0.0, acc_d[p])

    def f2_in(s, slot):
        t = s % tiles
        return [
            (token_rows(a2, t, TILE), rows_a.at[slot]), (token_rows(dy, t, TILE), rows_d.at[slot]),
            (token_cols(a2t, t, TILE), cols_a.at[slot]), (token_cols(dyt, t, TILE), cols_d.at[slot]),
        ]

    def f2_step(s, _):
        r, t, slot = s // tiles, s % tiles, s % 2
        m = blocks + r
        gather_ticks(m, t)

        @pl.when((t == 2) & (r >= 1))
        def _():
            reduce_middle(r - 1)

        @pl.when(t == 0)
        def _():
            loaded(m % 2)

        @pl.when(s + 1 < blocks * tiles)
        def _():
            start(f2_in(s + 1, 1 - slot), 1 - slot)

        wait(f2_in(s, slot), slot)
        w = wgu.at[m % 2]

        def products(c):
            at = pl.ds(c * CHUNK, CHUNK)
            a = rows_a[slot, at, :]
            return nn(a, w[0]), nn(a, w[1]), nn(rows_d[slot, at, :], wdt[...])

        def keep(c, values):
            at = pl.ds(c * CHUNK, CHUNK)
            act[at, :], dgu[0, at, :], dgu[1, at, :] = gated_back(*values)

        before = products(0)
        for c in range(1, TILE // CHUNK):
            now = products(c)
            keep(c - 1, before)
            before = now
        keep(TILE // CHUNK - 1, before)
        fold(r % 2, pl.ds(aligned(t * TILE, TILE), TILE), TILE, t == 0, r == 0, slot, w)

        @pl.when(t == tiles - 1)
        def _():
            @pl.when(r >= 1)
            def _():
                reduce_end(r - 1)

            reduce_start(r)

    start(f2_in(0, 0), 0)
    lax.fori_loop(0, blocks * tiles, f2_step, None)

    def back(slot, at, tok):
        da = total[:, tok].astype(BF).T.astype(F32)
        grad = norm_back(rows_a[slot, at, :], da).astype(BF).astype(F32)
        d = (rows_d[slot, at, :].astype(F32) + grad).astype(BF)
        rows_d[slot, at, :] = d
        return d

    def back_both(slot, at, tok):
        cols_d[slot, :, at] = back(slot, at, tok).T

    passes(
        lambda t, s: [(token_rows(h1, t, TILE), rows_a.at[s]), (token_rows(dy, t, TILE), rows_d.at[s])],
        lambda t, s: [(rows_d.at[s], token_rows(dh1, t, TILE)), (cols_d.at[s], token_cols(dh1t, t, TILE))],
        back_both,
    )

    def b1_in(s, slot):
        b, t = s // smalls, s % smalls
        some = pl.ds(0, SMALL)
        return [
            (token_rows(dh1, t, SMALL), rows_d.at[slot, some, :]),
            (token_cols(a1t, t, SMALL), cols_a.at[slot, :, some]), (token_cols(dh1t, t, SMALL), cols_d.at[slot, :, some]),
            (token_rows(g1.at[b], t, SMALL), g_buf.at[slot]), (token_rows(u1.at[b], t, SMALL), u_buf.at[slot]),
        ]

    def b1_step(s, _):
        b, t, slot = s // smalls, s % smalls, s % 2
        m, r = gathers + b, blocks + b

        @pl.when((t == 1) & (b + 1 < blocks))
        def _():
            load(b + 1, (m + 1) % 2)

        @pl.when(t == smalls // 2)
        def _():
            reduce_middle(r - 1)

        @pl.when(t == 0)
        def _():
            loaded(m % 2)

        @pl.when(s + 1 < blocks * smalls)
        def _():
            start(b1_in(s + 1, 1 - slot), 1 - slot)

        wait(b1_in(s, slot), slot)
        w = wgu.at[m % 2]
        for c in range(SMALL // CHUNK):
            at = pl.ds(c * CHUNK, CHUNK)
            d = nn(rows_d[slot, at, :], wdt[...])
            act[at, :], dgu[0, at, :], dgu[1, at, :] = gated_back(g_buf[slot, at, :], u_buf[slot, at, :], d)
        fold(r % 2, pl.ds(aligned(t * SMALL, SMALL), SMALL), SMALL, t == 0, b == 0, slot, w)

        @pl.when(t == smalls - 1)
        def _():
            reduce_end(r - 1)
            reduce_start(r)

    start(b1_in(0, 0), 0)
    lax.fori_loop(0, blocks * smalls, b1_step, None)

    last = layers * blocks - 1

    def leave(slot, at, tok):
        back(slot, at, tok)

    passes(
        lambda t, s: [(token_rows(x, t, TILE), rows_a.at[s]), (token_rows(dh1, t, TILE), rows_d.at[s])],
        lambda t, s: [(rows_d.at[s], token_rows(dx, t, TILE))],
        leave,
        [(2, lambda: reduce_middle(last))],
    )
    reduce_end(last)
    for copy in result_copies(last):
        copy.wait()
    for m in range(max(gathers - 4, 0), gathers):
        for k in range(5):
            sends_done(k, m)


def solution(mesh):
    n = mesh.shape["dp"]

    def local(x, dy, wg, wu, wd):
        tokens, width = x.shape[1:]
        layers, depth, ff = wg.shape
        span = n * LANES
        blocks = ff // span
        assert n == 4 and layers == 2 and mesh.shape["rep"] % 2 == 0
        assert ff % span == 0 and tokens % TILE == 0 and tokens // TILE == 4
        wide, tall = jax.ShapeDtypeStruct((tokens, width), BF), jax.ShapeDtypeStruct((width, tokens), BF)
        kept = jax.ShapeDtypeStruct((blocks, tokens, span), F32)
        grads = [jax.ShapeDtypeStruct(w.shape, w.dtype) for w in (wg, wu, wd)]
        hbm = [
            wide, tall, tall, wide, wide, tall, wide, tall, kept, kept,
            jax.ShapeDtypeStruct((layers * blocks, 2, width, span), BF), jax.ShapeDtypeStruct((layers * blocks, span, width), BF),
        ]
        outs = [wide, *grads, *hbm]
        dma = pltpu.SemaphoreType.DMA
        flops = 2 * tokens * width * ff * (9 * layers - 1)
        got = pl.pallas_call(
            functools.partial(kernel, n),
            out_shape=outs,
            in_specs=[pl.BlockSpec(memory_space=pl.ANY)] * 5,
            out_specs=[pl.BlockSpec(memory_space=pl.ANY)] * len(outs),
            scratch_shapes=[
                pltpu.VMEM((width, tokens), F32),
                pltpu.VMEM((2, 2, width, span), F32), pltpu.VMEM((2, width, span), F32),
                pltpu.VMEM((2, 2, width, span), BF), pltpu.VMEM((span, width), BF), pltpu.VMEM((width, span), BF),
                pltpu.VMEM((2, TILE, width), BF), pltpu.VMEM((2, TILE, width), BF),
                pltpu.VMEM((2, width, TILE), BF), pltpu.VMEM((2, width, TILE), BF),
                pltpu.VMEM((2, SMALL, span), F32), pltpu.VMEM((2, SMALL, span), F32),
                pltpu.VMEM((TILE, span), BF), pltpu.VMEM((2, TILE, span), BF),
                pltpu.VMEM((2, depth, span), BF), pltpu.VMEM((width, LANES), BF),
                pltpu.VMEM((2, depth, span), BF), pltpu.VMEM((width, LANES), BF),
                pltpu.VMEM((2, 2, depth, span), BF), pltpu.VMEM((2, width, LANES), BF),
                pltpu.VMEM((2, 2, depth, span), BF), pltpu.VMEM((2, width, LANES), BF),
                pltpu.VMEM((2, depth, span), BF), pltpu.VMEM((LANES, width), BF),
                dma((5, 2, 4)), dma((5, 2, layers * blocks)), dma((2,)), dma((5, 2)), dma((2, 2)), dma((3, 2)),
                dma((2, 2, 2)), dma((2, 2, 2)), dma((3, n)),
            ],
            compiler_params=pltpu.CompilerParams(collective_id=0, has_side_effects=True, vmem_limit_bytes=67043328),
            cost_estimate=pl.CostEstimate(flops=flops, bytes_accessed=0, transcendentals=0),
            name="stack",
        )(x[0], dy[0], wg, wu, wd)
        return (got[0][None], *got[1:4])

    tok, row = P(("rep", "dp"), None, None), P(None, "dp", None)
    return jax.shard_map(
        local, mesh=mesh, in_specs=(tok, tok, row, row, row), out_specs=(tok, *[P("rep", "dp", None)] * 3), check_vma=False
    )
```

time: 1330 us -> 689 us (0.52)
  Pallas kernels: 0 us -> 676 us
  matrix products: 657 us -> 0 us
  waiting for transfers between devices: 393 us -> 0 us
  other arithmetic: 212 us -> 0 us
  local copies, waits for them, and re-layouts: 42.8 us -> 12.7 us
  between operations: 14.6 us -> 0.66 us
    pallas_call x0 -> x1, Pallas kernels: none -> 676 us  [local(): pl.pallas_call(functools.partial(kernel, n), out_shape=outs, in_specs=[pl...]
    dot_general x17 -> x0, matrix products: 657 us -> none  [the longest x6 246 us: layer(): up = jnp.dot(a, w['w_up'], preferred_element_type=jnp.float32)]
    unnamed x18 -> x0, waiting for transfers between devices: 279 us -> none
    unnamed x4 -> x0, other arithmetic: 165 us -> none
    squeeze x6 -> x0, waiting for transfers between devices: 114 us -> none  [stack(): h = layer(h, {name: w[number] for name, w in weights.items()})]
    unnamed x33 -> x10, local copies, waits for them, and re-layouts: 33 us -> 12.7 us
    reshape x4 -> x0, other arithmetic: 18 us -> none  [the longest x1 12.3 us: step(): by_x.reshape(shape)]
  transfers between devices with their start and end apart: 12 -> 0, of which waited for: 8 -> 0; matrix products, arithmetic and copies ran while one was open for 52% -> 0% of each run, Pallas kernels for 0% -> 0%
where the time goes in v1:
time: 689 us
  Pallas kernels  676 us (98%)
  local copies, waits for them, and re-layouts  12.7 us (2%)
    pallas_call x1, Pallas kernels, local(): pl.pallas_call(functools.partial(kernel, n), out_shape=outs, in_specs=[pl...  676 us

profile of v1, /device:TPU:112, one launch (start us, length us, event | category | flops | bytes accessed | tf_op | source)
XLA Modules:
  0.0 689.0 jit_solution(14002502085387890674)
XLA Ops:
  0.6 675.7 %stack.1 = (bf16[4096,896]{1,0:T(8,128)(2,1)}, bf16[2,224,3584]{2,1,0:T(8,128)(2,1)}, bf16[2,224,3584]{2,1,0:T(8,128)(2,1)}, bf16[2,896,896]{2,1,0:T(8,128)(2,1)...) custom-call(bf16[4096,896]{1,0:T(8,128)(2,1)} %bitcast.4, ...), custom_call_target="tpu_custom_call" | custom-call | flops 447213469696 | tf_op jit(solution)/shard_map/stack/pallas_call | solution.py:582
  676.3 0.0 copy-start.2
  676.3 0.0 copy-start.1
  676.3 6.9 copy.13
  683.2 0.0 copy-done.2
  683.2 0.0 copy-start
  683.2 1.7 copy.14
  684.9 0.0 copy-done.1
  684.9 1.7 copy.15
  686.6 0.7 copy-done
  687.3 1.7 copy.16
Async XLA Ops:
  676.3 6.9 copy-start.2
  676.3 8.6 %copy-start.1 = (bf16[2,224,3584]{2,1,0:T(8,128)(2,1)S(1)}, bf16[2,224,3584]{2,1,0:T(8,128)(2,1)}, u32[]{:S(2)}) copy-start(bf16[2,224,3584]{2,1,0:T(8,128)(2,1)} %get-tuple-element.18) | copy-start | bytes 9633796
  683.2 4.1 copy-start

commit v2 on v1

v2 whole, which is shorter than its diff:
```python
import functools

import jax
import jax.numpy as jnp
from jax import lax
from jax.experimental import pallas as pl
from jax.experimental.pallas import tpu as pltpu
from jax.sharding import PartitionSpec as P

MESH = pl.DeviceIdType.MESH
BF, F32 = jnp.bfloat16, jnp.float32
LANES = 128
TILE = 1024
CHUNK = 256
STRIP = 256
SOON, LATER = (0,), (1, 2)
ALL = (0, 1, 2)
EPS = 1e-6


def nn(a, b):
    return jnp.dot(a, b, preferred_element_type=F32)


def nt(a, b):
    return lax.dot_general(a, b, (((1,), (1,)), ((), ())), preferred_element_type=F32)


def sigmoid(g):
    return 1.0 / (1.0 + jnp.exp(-g))


def gated_back(g, u, d):
    s = sigmoid(g)
    silu = g * s
    d = d.astype(BF).astype(F32)
    return (silu * u).astype(BF), ((d * u) * (s + silu * (1.0 - s))).astype(BF), (d * silu).astype(BF)


def kernel(
    n, x, dy, wg, wu, wd,
    dx, og, ou, od, a1, a1t, dyt, h1t, a2, a2t, dh1, dh1t, g1, u1, gw, gd,
    total, acc_w, acc_d, wgu, wdb, wdt, rows_a, rows_d, cols_a, cols_d, g_buf, u_buf, act, dgu,
    r1_w, r1_d, s2_w, s2_d, r2_w, r2_d, out_w, out_d,
    ag_send, ag_recv, load_sem, stream_sem, gu_sem, phase_sem, tall_sem, h1_sem, rs_send, rs_recv, out_sem,
):
    tokens, width = x.shape
    layers, depth, ff = wg.shape
    span = n * LANES
    share = ff // n
    blocks = ff // span
    tiles = tokens // TILE
    part_tile = TILE // 2
    half, dhalf = depth // 2, LANES // 2
    gathers = layers * blocks
    me = lax.axis_index("dp")
    rep = lax.axis_index("rep")
    core = rep % 2
    mate = rep + 1 - 2 * core
    right, left, across = (me + 1) % n, (me + n - 1) % n, (me + 2) % n
    to_right, to_left, to_mate = {"dp": right}, {"dp": left}, {"rep": mate}

    def aligned(v, m):
        return pl.multiple_of(v, m)

    def w_rows(owner, c):
        return pl.ds(aligned(owner * depth + c * half, 16), half)

    def d_rows(owner, c):
        return pl.ds(aligned(owner * LANES + c * dhalf, 16), dhalf)

    def remote(src, dst, send, recv, to):
        return pltpu.make_async_remote_copy(src_ref=src, dst_ref=dst, send_sem=send, recv_sem=recv, device_id=to, device_id_type=MESH)

    def wait_like(ref, sem):
        pltpu.make_async_copy(ref, ref, sem).wait()

    def piece(m, item, owner, part=None):
        if item < 2:
            return gw.at[m, item, w_rows(owner, core), pl.ds(0, span) if part is None else pl.ds(part * (span // 2), span // 2)]
        if part is None:
            return gd.at[m, d_rows(owner, core), :]
        return gd.at[m, pl.ds(aligned(owner * LANES + core * dhalf + part * (dhalf // 2), 16), dhalf // 2), :]

    def three_pieces(m, item):
        return gw.at[m, item, pl.ds(0, 3 * half), :] if item < 2 else gd.at[m, pl.ds(0, 3 * dhalf), :]

    def sends_done(k, m, items):
        for item in items:
            ref = three_pieces(m, item) if k == 4 else piece(m, item, me, None if k < 2 else 0)
            wait_like(ref, ag_send.at[k, item, m % 4])

    def give(m, items):
        layer, b = m // blocks, m % blocks

        @pl.when(m >= 4)
        def _():
            sends_done(0, m - 4, items)
            sends_done(1, m - 4, items)

        for item in items:
            for k, to in ((0, to_right), (1, to_left)):
                send, recv = ag_send.at[k, item, m % 4], ag_recv.at[k, item, m]
                if item == 2:
                    rows = pl.ds(aligned(b * LANES + core * dhalf, 16), dhalf)
                    remote(wd.at[layer, rows, :], piece(m, item, me), send, recv, to).start()
                    continue
                for group in range(n):
                    at = pl.ds(aligned(group * share + b * LANES, LANES), LANES)
                    remote(
                        (wg, wu)[item].at[layer, pl.ds(aligned(core * half, 16), half), at],
                        gw.at[m, item, w_rows(me, core), pl.ds(group * LANES, LANES)], send, recv, to,
                    ).start()

    def swap(m, owner, items):
        for item in items:
            ref = piece(m, item, owner)
            remote(ref, ref, ag_send.at[4, item, m % 4], ag_recv.at[4, item, m], to_mate).start()

    def pass_on(m, items):
        @pl.when(m >= 4)
        def _():
            for k in (2, 3, 4):
                sends_done(k, m - 4, items)

        for item in items:
            for k, owner, to in ((0, left, to_right), (1, right, to_left)):
                wait_like(piece(m, item, owner), ag_recv.at[k, item, m])
                ref = piece(m, item, owner, k)
                remote(ref, ref, ag_send.at[k + 2, item, m % 4], ag_recv.at[k + 2, item, m], to).start()
        swap(m, left, items)
        swap(m, right, items)

    def pass_across(m, items):
        for item in items:
            for part in range(2):
                wait_like(piece(m, item, across, part), ag_recv.at[part + 2, item, m])
        swap(m, across, items)

    def gathered(m):
        for item in ALL:
            wait_like(three_pieces(m, item), ag_recv.at[4, item, m])

    def load(m, slot):
        layer, b = m // blocks, m % blocks
        for owner in (left, right, across):
            r, d = pl.ds(aligned(owner * depth, 32), depth), pl.ds(aligned(owner * LANES, LANES), LANES)
            pltpu.make_async_copy(gw.at[m, :, r, :], wgu.at[slot, :, r, :], load_sem.at[0]).start()
            pltpu.make_async_copy(gd.at[m, d, :], wdb.at[d, :], load_sem.at[1]).start()
        r = pl.ds(aligned(me * depth, 32), depth)
        for j, w in enumerate((wg, wu)):
            for group in range(n):
                at = pl.ds(aligned(group * share + b * LANES, LANES), LANES)
                pltpu.make_async_copy(
                    w.at[layer, :, at], wgu.at[slot, j, r, pl.ds(group * LANES, LANES)], load_sem.at[0]
                ).start()
        pltpu.make_async_copy(
            wd.at[layer, pl.ds(aligned(b * LANES, LANES), LANES), :],
            wdb.at[pl.ds(aligned(me * LANES, LANES), LANES), :], load_sem.at[1],
        ).start()

    def loaded(slot):
        wait_like(wgu.at[slot], load_sem.at[0])
        wait_like(wdb, load_sem.at[1])
        for c in range(span // LANES):
            at = pl.ds(c * LANES, LANES)
            wdt[:, at] = wdb[at, :].T

    def gather_ticks(m, t):
        more = m + 1 < gathers
        first = m == 0

        @pl.when((t == 0) & more)
        def _():
            pass_on(m + 1, SOON)

        @pl.when((t == jnp.where(first, 1, 0)) & more)
        def _():
            pass_on(m + 1, LATER)

            @pl.when(m + 2 < gathers)
            def _():
                give(m + 2, ALL)

        @pl.when((t == jnp.where(first, 3, 2)) & more)
        def _():
            pass_across(m + 1, ALL)

        @pl.when(t == 3)
        def _():
            @pl.when(more)
            def _():
                gathered(m + 1)

            load((m + 1) % gathers, (m + 1) % 2)

    def own_w(p, j, owner, part=None):
        at = slice(None) if part is None else pl.ds(part * (span // 2), span // 2)
        return acc_w[p, j, pl.ds(aligned(owner * depth, 32), depth), at]

    def own_d(p, owner, part=None):
        at = slice(None) if part is None else pl.ds(part * (width // 2), width // 2)
        return acc_d[p, at, pl.ds(aligned(owner * LANES, LANES), LANES)]

    def item_half(ref_w, ref_d, item, part):
        if item < 2:
            return ref_w.at[item, :, pl.ds(part * (span // 2), span // 2)]
        return ref_d.at[pl.ds(part * (width // 2), width // 2), :]

    def first_copies(items):
        for item in items:
            for part, to in ((0, to_right), (1, to_left)):
                yield remote(
                    item_half(s2_w.at[1], s2_d.at[1], item, part), item_half(r1_w, r1_d, item, part),
                    rs_send.at[0, part, item], rs_recv.at[0, part, item], to,
                )

    def second_copies(items):
        for item in items:
            for part, to in ((0, to_right), (1, to_left)):
                src, dst = (s2_w.at[part, item], r2_w.at[part, item]) if item < 2 else (s2_d.at[part], r2_d.at[part])
                yield remote(src, dst, rs_send.at[1, part, item], rs_recv.at[1, part, item], to)

    def reduce_start(r):
        p = r % 2
        for j in range(2):
            s2_w[1, j] = own_w(p, j, across).astype(BF)
        s2_d[1] = own_d(p, across).astype(BF)
        for copy in first_copies(ALL):
            copy.start()

    def reduce_middle(r, items):
        p = r % 2
        for copy in first_copies(items):
            copy.wait()
        for part, owner in ((0, right), (1, left)):
            for j in items:
                size = (span if j < 2 else width) // 2
                came, plain = pl.ds(part * size, size), pl.ds((1 - part) * size, size)
                if j < 2:
                    s2_w[part, j, :, came] = (own_w(p, j, owner, part) + r1_w[j, :, came].astype(F32)).astype(BF)
                    s2_w[part, j, :, plain] = own_w(p, j, owner, 1 - part).astype(BF)
                else:
                    s2_d[part, came, :] = (own_d(p, owner, part) + r1_d[came, :].astype(F32)).astype(BF)
                    s2_d[part, plain, :] = own_d(p, owner, 1 - part).astype(BF)
        for copy in second_copies(items):
            copy.start()

    def result_copies(r):
        layer, b = layers - 1 - r // blocks, r % blocks
        for j, o in enumerate((og, ou)):
            for group in range(n):
                at = pl.ds(aligned(group * share + b * LANES, LANES), LANES)
                yield pltpu.make_async_copy(out_w.at[j, :, pl.ds(group * LANES, LANES)], o.at[layer, :, at], out_sem.at[j, group])
        yield pltpu.make_async_copy(out_d, od.at[layer, pl.ds(aligned(b * LANES, LANES), LANES), :], out_sem.at[2, 0])

    def reduce_end(r):
        p = r % 2
        for copy in second_copies(ALL):
            copy.wait()

        @pl.when(r >= 1)
        def _():
            for copy in result_copies(r - 1):
                copy.wait()

        for j in range(2):
            out_w[j] = (own_w(p, j, me) + r2_w[0, j].astype(F32) + r2_w[1, j].astype(F32)).astype(BF)
        mine = (own_d(p, me) + r2_d[0].astype(F32) + r2_d[1].astype(F32)).astype(BF)
        out_d[...] = mine.T
        for copy in result_copies(r):
            copy.start()

    def token_rows(ref, t):
        return ref.at[pl.ds(aligned(t * TILE, TILE), TILE), :]

    def token_cols(ref, t):
        return ref.at[:, pl.ds(aligned(t * TILE, TILE), TILE)]

    def half_cols(ref, t, h):
        return ref.at[:, pl.ds(aligned(t * TILE + h * part_tile, part_tile), part_tile)]

    def copies(pairs, slot, sem=stream_sem):
        for k, (src, dst) in enumerate(pairs):
            yield pltpu.make_async_copy(src, dst, sem.at[k, slot])

    def start(pairs, slot, sem=stream_sem):
        for copy in copies(pairs, slot, sem):
            copy.start()

    def wait(pairs, slot, sem=stream_sem):
        for copy in copies(pairs, slot, sem):
            copy.wait()

    def norm_scale(wide, axis):
        return lax.rsqrt(jnp.sum(wide * wide, axis, keepdims=True) * (1.0 / width) + EPS)

    def norm_back(h, da, axis):
        wide = h.astype(F32)
        scale = norm_scale(wide, axis)
        inner = jnp.sum(da * wide, axis, keepdims=True)
        return da * scale - wide * (scale * scale * scale * inner * (1.0 / width))

    def strips(t, h, body):
        def one(c, _):
            def at(first):
                return pl.ds(aligned(first + c * STRIP, STRIP), STRIP)

            body(at(0), at(h * part_tile), at(t * TILE + h * part_tile))

        lax.fori_loop(0, part_tile // STRIP, one, None)

    def passes(ins, outs, body, between):
        def tile(t, _):
            slot = t % 2
            wait(ins(t, slot), slot)
            strips(t, 0, functools.partial(body, slot))

            @pl.when(t >= 1)
            def _():
                wait(outs(t - 1, 1 - slot), 1 - slot, phase_sem)

            @pl.when(t + 1 < tiles)
            def _():
                start(ins(t + 1, 1 - slot), 1 - slot)

            strips(t, 1, functools.partial(body, slot))
            start(outs(t, slot), slot, phase_sem)
            for after, do in between:
                pl.when(t == after)(do)

        start(ins(0, 0), 0)
        lax.fori_loop(0, tiles, tile, None)

    barrier = pltpu.get_barrier_semaphore()
    for to in (to_right, to_left, to_mate):
        pl.semaphore_signal(barrier, inc=1, device_id=to, device_id_type=MESH)
    pl.semaphore_wait(barrier, 3)
    give(0, ALL)

    def enter(slot, part, at, _):
        wide = rows_a[slot, at, :].astype(F32)
        a = (wide * norm_scale(wide, 1)).astype(BF)
        rows_a[slot, at, :] = a
        cols_a[slot, :, at] = a.T
        cols_d[slot, :, at] = rows_d[slot, at, :].T

    def first_pass(items):
        pass_on(0, items)
        give(1, items)

    def first_load():
        pass_across(0, ALL)
        gathered(0)
        load(0, 0)

    def entered(t, slot):
        return [(rows_a.at[slot], token_rows(a1, t)), (cols_a.at[slot], token_cols(a1t, t)), (cols_d.at[slot], token_cols(dyt, t))]

    passes(
        lambda t, s: [(token_rows(x, t), rows_a.at[s]), (token_rows(dy, t), rows_d.at[s])], entered, enter,
        [(1, lambda: first_pass(SOON)), (2, lambda: first_pass(LATER)), (3, first_load)],
    )

    steps = blocks * tiles

    def add_total(at, first, value):
        total[:, at] = value + jnp.where(first, 0.0, total[:, at])

    def f1_in(s, slot):
        return [(token_rows(a1, s % tiles), rows_a.at[slot])]

    def gu_out(s, slot):
        m, t = s // tiles, s % tiles
        return [(g_buf.at[slot], token_rows(g1.at[m], t)), (u_buf.at[slot], token_rows(u1.at[m], t))]

    def f2_dy(t, slot):
        return [(token_rows(dy, t), rows_d.at[slot]), (token_cols(dyt, t), cols_d.at[slot])]

    def f2_first(t, slot):
        return [*f2_dy(t, slot), (token_rows(x, t), rows_a.at[slot])]

    def f2_in(t, slot):
        return [*f2_dy(t, slot), (token_rows(a2, t), rows_a.at[slot]), (token_cols(a2t, t), cols_a.at[slot])]

    def f1_step(s, _):
        m, t, slot = s // tiles, s % tiles, s % 2
        gather_ticks(m, t)

        @pl.when(t == 0)
        def _():
            loaded(m % 2)

        @pl.when(s == 0)
        def _():
            wait(entered(tiles - 1, (tiles - 1) % 2), (tiles - 1) % 2, phase_sem)

        @pl.when(s + 1 < steps)
        def _():
            start(f1_in(s + 1, 1 - slot), 1 - slot)

        @pl.when(s + 1 == steps)
        def _():
            start(f2_first(0, 0), 0)

        @pl.when(s >= 2)
        def _():
            wait(gu_out(s - 2, slot), slot, gu_sem)

        wait(f1_in(s, slot), slot)
        w = wgu.at[m % 2]
        for c in range(TILE // CHUNK):
            at = pl.ds(c * CHUNK, CHUNK)
            a = rows_a[slot, at, :]
            g, u = nn(a, w[0]), nn(a, w[1])
            g_buf[slot, at, :] = g
            u_buf[slot, at, :] = u
            act[at, :] = (g * sigmoid(g) * u).astype(BF)
        start(gu_out(s, slot), slot, gu_sem)
        add_total(pl.ds(aligned(t * TILE, TILE), TILE), m == 0, nt(wdt[...], act[...]))

    start(f1_in(0, 0), 0)
    lax.fori_loop(0, steps, f1_step, None)
    for s in (steps - 2, steps - 1):
        wait(gu_out(s, s % 2), s % 2, gu_sem)

    def fold_states(c, size, t, first_block, w):
        at = pl.ds(c * size, size)
        add_total(pl.ds(aligned(t * TILE + c * size, size), size), first_block, nt(w[0], dgu[0, at, :]) + nt(w[1], dgu[1, at, :]))

    def fold(p, first_step, slot):
        for j in range(2):
            acc_w[p, j] = nn(cols_a[slot], dgu[j]) + jnp.where(first_step, 0.0, acc_w[p, j])
        acc_d[p] = nn(cols_d[slot], act[...]) + jnp.where(first_step, 0.0, acc_d[p])

    def h1_out(t, h):
        for i in range(n):
            rows = h1t.at[pl.ds(i * depth, depth), :]
            yield pltpu.make_async_copy((s2_w, r2_w)[h].at[i // 2, i % 2], half_cols(rows, t, h), h1_sem.at[h, i])

    def f2_out(t, slot):
        return [(rows_a.at[slot], token_rows(a2, t)), (cols_a.at[slot], token_cols(a2t, t))]

    def turn(slot, h, part, at, tok):
        state = (rows_a[slot, at, :].T.astype(F32) + total[:, tok].astype(BF).astype(F32)).astype(BF)
        for i in range(n):
            (s2_w, r2_w)[h][i // 2, i % 2, :, part] = state[i * depth : (i + 1) * depth, :]
        wide = state.astype(F32)
        a = (wide * norm_scale(wide, 0)).astype(BF)
        cols_a[slot, :, at] = a
        rows_a[slot, at, :] = a.T

    def b1_more(s, slot):
        b, t = s // tiles, s % tiles
        return [
            (token_cols(a1t, t), cols_a.at[slot]),
            (token_rows(g1.at[b], t), g_buf.at[slot]), (token_rows(u1.at[b], t), u_buf.at[slot]),
        ]

    def b1_first(s, slot):
        return [*b1_more(s, slot), (token_cols(dyt, s % tiles), cols_d.at[slot])]

    def h1_in(t, h):
        return pltpu.make_async_copy(half_cols(h1t, t, h), rows_a.at[h, pl.ds(0, width), pl.ds(0, part_tile)], tall_sem.at[h])

    def f2_step(s, _):
        r, t, slot = s // tiles, s % tiles, s % 2
        m = blocks + r
        gather_ticks(m, t)

        @pl.when((t == 1) & (r >= 1))
        def _():
            reduce_middle(r - 1, SOON)

        @pl.when((t == 2) & (r >= 1))
        def _():
            reduce_middle(r - 1, LATER)

        @pl.when(t == 0)
        def _():
            loaded(m % 2)

        @pl.when((s >= 1) & (s <= tiles))
        def _():
            wait(f2_out(s - 1, 1 - slot), 1 - slot, phase_sem)

        @pl.when(s + 1 < tiles)
        def _():
            start(f2_first(t + 1, 1 - slot), 1 - slot)

        @pl.when((s + 1 >= tiles) & (s + 1 < steps))
        def _():
            start(f2_in((s + 1) % tiles, 1 - slot), 1 - slot)

        @pl.when(s + 1 == steps)
        def _():
            h1_in(0, 0).start()
            start(b1_first(0, 0), 0)

        @pl.when(r == 0)
        def _():
            wait(f2_first(t, slot), slot)
            for h in range(2):
                @pl.when(t >= 1)
                def _():
                    for copy in h1_out(t - 1, h):
                        copy.wait()

                strips(t, h, functools.partial(turn, slot, h))
                for copy in h1_out(t, h):
                    copy.start()
            start(f2_out(t, slot), slot, phase_sem)

        @pl.when(r >= 1)
        def _():
            wait(f2_in(t, slot), slot)

        w = wgu.at[m % 2]

        def products(c):
            at = pl.ds(c * CHUNK, CHUNK)
            a = rows_a[slot, at, :]
            return nn(a, w[0]), nn(a, w[1]), nn(rows_d[slot, at, :], wdt[...])

        def keep(c, values):
            at = pl.ds(c * CHUNK, CHUNK)
            act[at, :], dgu[0, at, :], dgu[1, at, :] = gated_back(*values)

        before = products(0)
        for c in range(1, TILE // CHUNK):
            now = products(c)
            keep(c - 1, before)
            before = now
        keep(TILE // CHUNK - 1, before)
        for h in range(2):
            fold_states(h, part_tile, t, r == 0, w)
        fold(r % 2, t == 0, slot)

        @pl.when(t == tiles - 1)
        def _():
            @pl.when(r == 0)
            def _():
                for h in range(2):
                    for copy in h1_out(t, h):
                        copy.wait()

            @pl.when(r >= 1)
            def _():
                reduce_end(r - 1)

            reduce_start(r)

    lax.fori_loop(0, steps, f2_step, None)

    def b1_in(s, slot):
        t = s % tiles
        return [*b1_more(s, slot), (token_cols(dh1t, t), cols_d.at[slot]), (token_rows(dh1, t), rows_d.at[slot])]

    def b1_out(t, slot):
        return [(rows_d.at[slot], token_rows(dh1, t)), (cols_d.at[slot], token_cols(dh1t, t))]

    def back(state, grad, da, axis):
        through = norm_back(state, da.astype(F32), axis)
        return (grad.astype(F32) + through.astype(BF).astype(F32)).astype(BF)

    def turn_back(slot, h, part, at, tok):
        d = back(rows_a[h, pl.ds(0, width), part], cols_d[slot, :, at], total[:, tok].astype(BF), 0)
        cols_d[slot, :, at] = d
        rows_d[slot, at, :] = d.T

    def b1_body(slot, b, t, w, states, weights):
        def product(c):
            return nn(rows_d[slot, pl.ds(c * CHUNK, CHUNK), :], wdt[...])

        def keep(c, d):
            at = pl.ds(c * CHUNK, CHUNK)
            act[at, :], dgu[0, at, :], dgu[1, at, :] = gated_back(g_buf[slot, at, :], u_buf[slot, at, :], d)
            if states:
                fold_states(c, CHUNK, t, b == 0, w)

        before = product(0)
        for c in range(1, TILE // CHUNK):
            now = product(c)
            keep(c - 1, before)
            before = now
        keep(TILE // CHUNK - 1, before)
        if weights:
            fold((blocks + b) % 2, t == 0, slot)

    def end_in(t, slot):
        return [
            (token_rows(x, t), rows_a.at[slot]),
            (token_rows(g1.at[blocks - 1], t), g_buf.at[slot]), (token_rows(u1.at[blocks - 1], t), u_buf.at[slot]),
        ]

    def end_rows(t, slot):
        return pltpu.make_async_copy(token_rows(dh1, t), rows_d.at[slot], tall_sem.at[slot])

    def b1_step(final, s, _):
        b, t, slot = s // tiles, s % tiles, s % 2
        m, r = gathers + b, blocks + b

        @pl.when((t == 1) & (b + 1 < blocks))
        def _():
            load(b + 1, (m + 1) % 2)

        @pl.when(t == 1)
        def _():
            reduce_middle(r - 1, SOON)

        @pl.when(t == 2)
        def _():
            reduce_middle(r - 1, LATER)

        @pl.when(t == 0)
        def _():
            loaded(m % 2)

        if not final:
            @pl.when((s >= 1) & (s <= tiles))
            def _():
                wait(b1_out(s - 1, 1 - slot), 1 - slot, phase_sem)

            @pl.when(s + 1 < tiles)
            def _():
                start(b1_first(s + 1, 1 - slot), 1 - slot)

        @pl.when((s + 1 >= tiles) & (s + 1 < steps))
        def _():
            start(b1_in(s + 1, 1 - slot), 1 - slot)

        if final:
            @pl.when(s + 1 == steps)
            def _():
                start(end_in(0, 0), 0)
                end_rows(0, 0).start()

            wait(b1_in(s, slot), slot)
        else:
            @pl.when(b == 0)
            def _():
                wait(b1_first(s, slot), slot)
                for h in range(2):
                    h1_in(t, h).wait()
                    strips(t, h, functools.partial(turn_back, slot, h))

                    @pl.when(t + 1 < tiles)
                    def _():
                        h1_in(t + 1, h).start()

                start(b1_out(t, slot), slot, phase_sem)

            @pl.when(b >= 1)
            def _():
                wait(b1_in(s, slot), slot)

        b1_body(slot, b, t, wgu.at[m % 2], not final, True)

        @pl.when(t == tiles - 1)
        def _():
            reduce_end(r - 1)
            reduce_start(r)

    h1_in(0, 1).start()
    lax.fori_loop(0, steps - tiles, functools.partial(b1_step, False), None)
    lax.fori_loop(steps - tiles, steps, functools.partial(b1_step, True), None)

    last = layers * blocks - 1

    def leave(slot, part, at, tok):
        rows_d[slot, at, :] = back(rows_a[slot, at, :], rows_d[slot, at, :], total[:, tok].astype(BF).T, 1)

    def left_out(t, slot):
        return [(rows_d.at[slot], token_rows(dx, t))]

    def end_step(t, _):
        slot = t % 2

        @pl.when(t + 1 < tiles)
        def _():
            start(end_in(t + 1, 1 - slot), 1 - slot)

        wait(end_in(t, slot), slot)
        end_rows(t, slot).wait()
        b1_body(slot, blocks - 1, t, wgu.at[(gathers + blocks - 1) % 2], True, False)

        @pl.when(t >= 1)
        def _():
            wait(left_out(t - 1, 1 - slot), 1 - slot, phase_sem)

        @pl.when(t + 1 < tiles)
        def _():
            end_rows(t + 1, 1 - slot).start()

        for h in range(2):
            strips(t, h, functools.partial(leave, slot))
        start(left_out(t, slot), slot, phase_sem)

        @pl.when(t == 0)
        def _():
            reduce_middle(last, SOON)

        @pl.when(t == 1)
        def _():
            reduce_middle(last, LATER)

    lax.fori_loop(0, tiles, end_step, None)
    wait(left_out(tiles - 1, (tiles - 1) % 2), (tiles - 1) % 2, phase_sem)
    reduce_end(last)
    for copy in result_copies(last):
        copy.wait()
    for m in range(max(gathers - 4, 0), gathers):
        for k in range(5):
            sends_done(k, m, ALL)


def solution(mesh):
    n = mesh.shape["dp"]

    def local(x, dy, wg, wu, wd):
        tokens, width = x.shape[1:]
        layers, depth, ff = wg.shape
        span = n * LANES
        blocks = ff // span
        assert n == 4 and layers == 2 and mesh.shape["rep"] % 2 == 0
        assert ff % span == 0 and tokens % TILE == 0 and tokens // TILE == 4
        wide, tall = jax.ShapeDtypeStruct((tokens, width), BF), jax.ShapeDtypeStruct((width, tokens), BF)
        kept = jax.ShapeDtypeStruct((blocks, tokens, span), F32)
        grads = [jax.ShapeDtypeStruct(w.shape, w.dtype) for w in (wg, wu, wd)]
        hbm = [
            wide, tall, tall, tall, wide, tall, wide, tall, kept, kept,
            jax.ShapeDtypeStruct((layers * blocks, 2, width, span), BF), jax.ShapeDtypeStruct((layers * blocks, span, width), BF),
        ]
        outs = [wide, *grads, *hbm]
        dma = pltpu.SemaphoreType.DMA
        flops = 2 * tokens * width * ff * (9 * layers - 1)
        got = pl.pallas_call(
            functools.partial(kernel, n),
            out_shape=outs,
            in_specs=[pl.BlockSpec(memory_space=pl.ANY)] * 5,
            out_specs=[pl.BlockSpec(memory_space=pl.ANY)] * len(outs),
            scratch_shapes=[
                pltpu.VMEM((width, tokens), F32),
                pltpu.VMEM((2, 2, width, span), F32), pltpu.VMEM((2, width, span), F32),
                pltpu.VMEM((2, 2, width, span), BF), pltpu.VMEM((span, width), BF), pltpu.VMEM((width, span), BF),
                pltpu.VMEM((2, TILE, width), BF), pltpu.VMEM((2, TILE, width), BF),
                pltpu.VMEM((2, width, TILE), BF), pltpu.VMEM((2, width, TILE), BF),
                pltpu.VMEM((2, TILE, span), F32), pltpu.VMEM((2, TILE, span), F32),
                pltpu.VMEM((TILE, span), BF), pltpu.VMEM((2, TILE, span), BF),
                pltpu.VMEM((2, depth, span), BF), pltpu.VMEM((width, LANES), BF),
                pltpu.VMEM((2, 2, depth, span), BF), pltpu.VMEM((2, width, LANES), BF),
                pltpu.VMEM((2, 2, depth, span), BF), pltpu.VMEM((2, width, LANES), BF),
                pltpu.VMEM((2, depth, span), BF), pltpu.VMEM((LANES, width), BF),
                dma((5, 3, 4)), dma((5, 3, layers * blocks)), dma((2,)), dma((5, 2)), dma((2, 2)), dma((5, 2)), dma((2,)), dma((2, n)),
                dma((2, 2, 3)), dma((2, 2, 3)), dma((3, n)),
            ],
            compiler_params=pltpu.CompilerParams(collective_id=0, has_side_effects=True, vmem_limit_bytes=67043328),
            cost_estimate=pl.CostEstimate(flops=flops, bytes_accessed=0, transcendentals=0),
            name="stack",
        )(x[0], dy[0], wg, wu, wd)
        return (got[0][None], *got[1:4])

    tok, row = P(("rep", "dp"), None, None), P(None, "dp", None)
    return jax.shard_map(
        local, mesh=mesh, in_specs=(tok, tok, row, row, row), out_specs=(tok, *[P("rep", "dp", None)] * 3), check_vma=False
    )
```

time: 689 us -> 635 us (0.922)
  Pallas kernels: 676 us -> 622 us
    pallas_call x1, Pallas kernels: 676 us -> 622 us  [local(): pl.pallas_call(functools.partial(kernel, n), out_shape=outs, in_specs=[pl...]
where the time goes in v2:
time: 635 us
  Pallas kernels  622 us (98%)
  local copies, waits for them, and re-layouts  12.7 us (2%)
    pallas_call x1, Pallas kernels, local(): pl.pallas_call(functools.partial(kernel, n), out_shape=outs, in_specs=[pl...  622 us

profile of v2, /device:TPU:112, one launch (start us, length us, event | category | flops | bytes accessed | tf_op | source)
XLA Modules:
  0.0 635.2 jit_solution(14292849075514631663)
XLA Ops:
  0.6 621.8 %stack.1 = (bf16[4096,896]{1,0:T(8,128)(2,1)}, bf16[2,224,3584]{2,1,0:T(8,128)(2,1)}, bf16[2,224,3584]{2,1,0:T(8,128)(2,1)}, bf16[2,896,896]{2,1,0:T(8,128)(2,1)...) custom-call(bf16[4096,896]{1,0:T(8,128)(2,1)} %bitcast.4, ...), custom_call_target="tpu_custom_call" | custom-call | flops 447213469696 | tf_op jit(solution)/shard_map/stack/pallas_call | solution.py:737
  622.5 0.0 copy-start.2
  622.5 0.0 copy-start.1
  622.5 6.9 %copy.13 = bf16[1,4096,896]{2,1,0:T(8,128)(2,1)} copy(bf16[1,4096,896]{2,1,0:T(8,128)(2,1)} %bitcast.3) | data formatting | bytes 14680064
  629.4 0.0 copy-done.2
  629.4 0.0 copy-start
  629.4 1.7 copy.14
  631.1 0.0 copy-done.1
  631.1 1.7 copy.15
  632.8 0.7 copy-done
  633.5 1.7 copy.16
Async XLA Ops:
  622.5 6.9 %copy-start.2 = (bf16[2,224,3584]{2,1,0:T(8,128)(2,1)S(1)}, bf16[2,224,3584]{2,1,0:T(8,128)(2,1)}, u32[]{:S(2)}) copy-start(bf16[2,224,3584]{2,1,0:T(8,128)(2,1)} %get-tuple-element.17) | copy-start | bytes 9633796
  622.5 8.6 %copy-start.1 = (bf16[2,224,3584]{2,1,0:T(8,128)(2,1)S(1)}, bf16[2,224,3584]{2,1,0:T(8,128)(2,1)}, u32[]{:S(2)}) copy-start(bf16[2,224,3584]{2,1,0:T(8,128)(2,1)} %get-tuple-element.18) | copy-start | bytes 9633796
  629.4 4.1 copy-start
